TPU v7x, 32 devices: a whole 2x2x4 slice. The times are simulated.
32 devices in a mesh: seq: 8 (over z, x), fsdp: 4 (over y, core).
Axes of the slice: x: 2, y: 2, z: 4, core: 2. Of those that a mesh axis runs over, the one named last changes fastest.
Arguments:
- tokens: bfloat16 [4, 1024, 2048], P('fsdp', 'seq'), may hold values from -6 to 6
- cotangent: bfloat16 [4, 1024, 2048], P('fsdp', 'seq'), may hold values from -6 to 6
- routes: int32 [4, 1024, 8], P('fsdp', 'seq'), may hold values from 0 to 63, all different within a row; in each aligned block of 128 rows (0 to 127, 128 to 255, ..., all dimensions but the last counted through in order) at most 32 rows name the same one
- norm1_gain: bfloat16 [2048], P(('seq', 'fsdp')), may hold values from 0.099609375 to 1.8984375
- query_weight: bfloat16 [2048, 2048], P(('seq', 'fsdp')), may hold values from -0.125 to 0.125
- key_weight: bfloat16 [2048, 2048], P(('seq', 'fsdp')), may hold values from -0.125 to 0.125
- value_weight: bfloat16 [2048, 2048], P(('seq', 'fsdp')), may hold values from -0.125 to 0.125
- output_weight: bfloat16 [2048, 2048], P(('seq', 'fsdp')), may hold values from -2 to 2
- norm2_gain: bfloat16 [2048], P(('seq', 'fsdp')), may hold values from 0.099609375 to 1.8984375
- router_weight: bfloat16 [2048, 64], P(('seq', 'fsdp')), may hold values from -0.125 to 0.125
- expert_gate: bfloat16 [128, 2048, 512], P(('seq', 'fsdp')), may hold values from -0.125 to 0.125
- expert_up: bfloat16 [128, 2048, 512], P(('seq', 'fsdp')), may hold values from -0.125 to 0.125
- expert_down: bfloat16 [128, 512, 2048], P(('seq', 'fsdp')), may hold values from -0.75 to 0.75
Outputs:
- block_out: bfloat16 [4, 1024, 2048], P('fsdp', 'seq')
- input_grad: float32 [4, 1024, 2048], P('fsdp', 'seq')
- norm1_gain_grad: float32 [2048], P(('seq', 'fsdp'))
- query_weight_grad: float32 [2048, 2048], P(('seq', 'fsdp'))
- key_weight_grad: float32 [2048, 2048], P(('seq', 'fsdp'))
- value_weight_grad: float32 [2048, 2048], P(('seq', 'fsdp'))
- output_weight_grad: float32 [2048, 2048], P(('seq', 'fsdp'))
- norm2_gain_grad: float32 [2048], P(('seq', 'fsdp'))
- router_weight_grad: float32 [2048, 64], P(('seq', 'fsdp'))
- expert_gate_grad: float32 [128, 2048, 512], P(('seq', 'fsdp'))
- expert_up_grad: float32 [128, 2048, 512], P(('seq', 'fsdp'))
- expert_down_grad: float32 [128, 512, 2048], P(('seq', 'fsdp'))
Inputs may be any that keep to these rules, and one draw needn't show every extreme that they name: `routes`: each row names 8 different experts. Among the 128 rows of one device (aligned blocks of the flattened sequences) no expert is named more than 32 times, and in every draw some expert is named exactly 32 times in some block; every expert is named somewhere.
All inputs are finite; a program needn't handle non-finite values.
Results may differ from a plain program's by a relative error of at most 0.02.
Values may be sent and summed in bfloat16 or wider, within the bound.
A program may use at most 448 MiB of HBM per device.

v0:
```python
import jax
import jax.numpy as jnp
from jax import lax
from jax.sharding import PartitionSpec as P

H = 16
HD = 128
SPLIT = 2
AXES = ("seq", "fsdp")
epsilon = 1e-06
rope_base = 50000.0
bf16 = jnp.bfloat16
f32 = jnp.float32


def norm_rows(values, scales):
    mean_sq = jnp.mean(values * values, axis=-1, keepdims=True)
    return values * lax.rsqrt(mean_sq + epsilon) * scales


def rope_tables(positions, head_dim):
    half_dim = head_dim // 2
    frequency = rope_base ** (-(2.0 * jnp.arange(half_dim, dtype=f32)) / head_dim)
    angles = positions.astype(f32)[:, None] * frequency[None, :]
    return (jnp.cos(angles), jnp.sin(angles))


def rotate(values, cosine, sine_tab, inverse):
    half_dim = values.shape[-1] // 2
    low_half = values[..., :half_dim]
    high_half = values[..., half_dim:]
    cos_rows = cosine[:, None, :]
    sin_rows = -sine_tab[:, None, :] if inverse else sine_tab[:, None, :]
    return jnp.concatenate(
        [low_half * cos_rows - high_half * sin_rows, high_half * cos_rows + low_half * sin_rows],
        axis=-1,
    )


def route_weights(logits, chosen):
    expo = jnp.exp(logits)
    probability = expo / jnp.sum(expo, axis=-1, keepdims=True)
    experts = jnp.arange(logits.shape[1], dtype=jnp.int32)
    match = (chosen[:, :, None] == experts).astype(f32)
    picked = jnp.sum(match * probability[:, None, :], axis=-1)
    return picked / jnp.sum(picked, axis=-1, keepdims=True)


def mm(left, right):
    return jnp.dot(left, right, preferred_element_type=f32)


def mm_tn(left, right):
    return lax.dot_general(left, right, (((0,), (0,)), ((), ())), preferred_element_type=f32)


def mm_nt(left, right):
    return lax.dot_general(left, right, (((1,), (1,)), ((), ())), preferred_element_type=f32)


def ein(spec, *args):
    return jnp.einsum(spec, *args, preferred_element_type=f32)


def body(
    tokens,
    cotangent,
    routes,
    norm1_gain,
    query_weight,
    key_weight,
    value_weight,
    output_weight,
    norm2_gain,
    router_weight,
    expert_gate,
    expert_up,
    expert_down,
):
    n_seq = lax.axis_size("seq")
    n_fsdp = lax.axis_size("fsdp")
    n_dev = n_seq * n_fsdp
    seq_at = lax.axis_index("seq")
    dev_at = seq_at * n_fsdp + lax.axis_index("fsdp")
    tok_rows, width = (tokens.shape[1], tokens.shape[2])
    length = tok_rows * n_seq
    heads = H // n_seq
    cols = heads * HD
    shard = query_weight.shape[0]
    experts = router_weight.shape[1]
    top_k = routes.shape[2]
    capacity = tok_rows * top_k // experts * 2
    pieces = expert_gate.shape[0]
    n_loc = max(1, pieces // SPLIT)
    per_loc = pieces // n_loc
    first_expert = dev_at * pieces // SPLIT
    x_own = tokens[0]
    cot_own = cotangent[0]
    chosen = routes[0]
    routes_all = lax.all_gather(chosen, AXES, axis=0, tiled=True)
    x_seq = lax.all_gather(x_own, "seq", axis=0, tiled=True)
    small = jnp.concatenate(
        [
            router_weight,
            norm1_gain[:, None],
            norm2_gain[:, None],
            jnp.zeros((shard, 128 - experts - 2), bf16),
        ],
        axis=1,
    )
    blocks = jnp.concatenate(
        [
            query_weight.reshape(shard, n_seq, cols),
            key_weight.reshape(shard, n_seq, cols),
            value_weight.reshape(shard, n_seq, cols),
            jnp.broadcast_to(small[:, None, :], (shard, n_seq, 128)),
        ],
        axis=2,
    ).transpose(1, 0, 2)
    moved = lax.all_to_all(blocks, "seq", split_axis=0, concat_axis=0, tiled=True)
    packed = lax.all_gather(moved, "fsdp", axis=1).reshape(width, 3 * cols + 128)
    w_qkv = packed[:, : 3 * cols]
    router_full = packed[:, 3 * cols : 3 * cols + experts]
    gain_in = packed[:, 3 * cols + experts].astype(f32)
    gain_mid = packed[:, 3 * cols + experts + 1].astype(f32)
    out_full = lax.all_gather(output_weight, AXES, axis=0, tiled=True)
    out_rows = lax.dynamic_slice_in_dim(out_full, seq_at * cols, cols, 0)
    cot_all = lax.all_gather(cot_own, AXES, axis=0, tiled=True)
    cosine, sine_tab = rope_tables(jnp.arange(length, dtype=jnp.int32), HD)
    normed_in = norm_rows(x_seq.astype(f32), gain_in).astype(bf16)
    qkv = mm(normed_in, w_qkv)
    q = rotate(qkv[:, :cols].reshape(length, heads, HD), cosine, sine_tab, False).astype(bf16)
    k = rotate(qkv[:, cols : 2 * cols].reshape(length, heads, HD), cosine, sine_tab, False).astype(
        bf16
    )
    v = qkv[:, 2 * cols :].astype(bf16).reshape(length, heads, HD)
    scale = HD ** (-0.5)
    scores = ein("qhd,khd->hqk", q, k) * scale
    totals = jnp.log(jnp.sum(jnp.exp(scores), axis=-1))
    probs = jnp.exp(scores - totals[..., None])
    attn_heads = ein("hqk,khd->qhd", probs.astype(bf16), v).astype(bf16)
    attn_flat = attn_heads.reshape(length, cols)
    attn_rows = lax.all_to_all(attn_flat, "seq", split_axis=0, concat_axis=1, tiled=True)
    x_own32 = x_own.astype(f32)
    residual = x_own32 + mm(attn_rows, out_full)
    normed_mid = norm_rows(residual, gain_mid).astype(bf16)
    x_all = lax.all_gather(normed_mid, AXES, axis=0, tiled=True)
    logits_all = mm(x_all, router_full)
    w_all = route_weights(logits_all, routes_all)
    local = first_expert + jnp.arange(n_loc, dtype=jnp.int32)
    match = routes_all.reshape(n_dev, tok_rows, top_k)[:, None] == local[None, :, None, None]
    hit = jnp.any(match, axis=-1)
    w_hit = jnp.sum(jnp.where(match, w_all.reshape(n_dev, 1, tok_rows, top_k), 0.0), axis=-1)
    tri = (jnp.arange(tok_rows)[:, None] <= jnp.arange(tok_rows)[None, :]).astype(bf16)
    place = ein("bet,tu->beu", hit.astype(bf16), tri).astype(jnp.int32) - 1
    slots = jnp.arange(capacity, dtype=jnp.int32)
    pick = hit[:, :, None, :] & (place[:, :, None, :] == slots[None, None, :, None])
    one = pick.astype(bf16)
    w_slot = jnp.sum(jnp.where(pick, w_hit[:, :, None, :], 0.0), axis=-1)
    rows_of = lambda a: ein("best,btd->ebsd", one, a.reshape(n_dev, tok_rows, width)).reshape(
        n_loc, n_dev * capacity, width
    )
    rows_in = rows_of(x_all).astype(bf16)
    rows_cot = rows_of(cot_all)
    w_rows = w_slot.transpose(1, 0, 2).reshape(n_loc, n_dev * capacity, 1)
    rows_grad = (w_rows * rows_cot).astype(bf16)
    gate = expert_gate.reshape(n_loc, per_loc, width, -1)
    up = expert_up.reshape(n_loc, per_loc, width, -1)
    down = expert_down.reshape(n_loc, per_loc, -1, width)
    pre_gate = ein("erd,epdf->eprf", rows_in, gate)
    pre_up = ein("erd,epdf->eprf", rows_in, up)
    sig = jax.nn.sigmoid(pre_gate)
    active = pre_gate * sig
    hidden = (active * pre_up).astype(bf16)
    hidden_grad = ein("erd,epfd->eprf", rows_grad, down)
    gate_grad = (hidden_grad * pre_up * sig * (1.0 + pre_gate * (1.0 - sig))).astype(bf16)
    up_grad = (hidden_grad * active).astype(bf16)
    back = ein("eprf,epdf->erd", gate_grad, gate) + ein("eprf,epdf->erd", up_grad, up)
    out = ein("eprf,epfd->erd", hidden, down)
    w_back = jnp.sum(rows_cot * out, axis=-1)
    spread = (
        lambda a: ein("best,ebsd->btd", one, a.astype(bf16).reshape(n_loc, n_dev, capacity, width))
        .astype(bf16)
        .reshape(n_dev * tok_rows, width)
    )
    back_own = lax.psum_scatter(spread(back), AXES, scatter_dimension=0, tiled=True)
    w_tok = jnp.sum(
        jnp.where(pick, w_back.reshape(n_loc, n_dev, capacity).transpose(1, 0, 2)[..., None], 0.0),
        axis=2,
    )
    w_parts = lax.all_to_all(w_tok, AXES, split_axis=0, concat_axis=0, tiled=True)
    w_by_expert = w_parts.reshape(experts, n_dev * n_loc // experts, tok_rows).sum(axis=1)
    own_match = (chosen[:, :, None] == jnp.arange(experts, dtype=jnp.int32)).astype(f32)
    weight_grad = jnp.sum(own_match * w_by_expert.T[:, None, :], axis=-1)
    moe_own = lax.psum_scatter(spread(w_rows * out), AXES, scatter_dimension=0, tiled=True)
    block_out = (residual + moe_own.astype(f32)).astype(bf16)
    down_grad = ein("eprf,erd->epfd", hidden, rows_grad).reshape(expert_down.shape)
    gate_weight_grad = ein("erd,eprf->epdf", rows_in, gate_grad).reshape(expert_gate.shape)
    up_weight_grad = ein("erd,eprf->epdf", rows_in, up_grad).reshape(expert_up.shape)
    logits = mm(normed_mid, router_full)
    _, route_back = jax.vjp(lambda values: route_weights(values, chosen), logits)
    logit_grad = route_back(weight_grad)[0].astype(bf16)
    normed_total = back_own.astype(f32) + mm_nt(logit_grad, router_full)
    logit_all = lax.all_gather(logit_grad, AXES, axis=0, tiled=True)
    x_cols = lax.dynamic_slice_in_dim(x_all, dev_at * shard, shard, 1)
    grad_router = mm_tn(x_cols, logit_all)
    cot32 = cot_own.astype(f32)
    _, norm_back = jax.vjp(norm_rows, residual, gain_mid)
    resid_part, gain_two = norm_back(normed_total)
    resid_grad = cot32 + resid_part
    resid_seq = lax.all_gather(resid_grad.astype(bf16), "seq", axis=0, tiled=True)
    grad_out_rows = mm_tn(attn_flat, resid_seq)
    grad_output = lax.psum_scatter(grad_out_rows, "fsdp", scatter_dimension=0, tiled=True)
    attn_grad = mm_nt(resid_seq, out_rows).astype(bf16).reshape(length, heads, HD)
    delta = jnp.sum(attn_grad.astype(f32) * attn_heads.astype(f32), axis=-1)
    v_grad = ein("hqk,qhd->khd", probs.astype(bf16), attn_grad).astype(bf16)
    p_grad = ein("qhd,khd->hqk", attn_grad, v)
    s_grad = (probs * (p_grad - delta.T[:, :, None]) * scale).astype(bf16)
    q_grad = ein("hqk,khd->qhd", s_grad, k).astype(bf16)
    k_grad = ein("hqk,qhd->khd", s_grad, q).astype(bf16)
    q_rows = rotate(q_grad.astype(f32), cosine, sine_tab, True).astype(bf16)
    k_rows = rotate(k_grad.astype(f32), cosine, sine_tab, True).astype(bf16)
    d_qkv = jnp.concatenate([a.reshape(length, cols) for a in (q_rows, k_rows, v_grad)], axis=1)
    in_part = mm_nt(d_qkv, w_qkv).astype(bf16)
    normed_in_grad = lax.psum_scatter(in_part, "seq", scatter_dimension=0, tiled=True).astype(f32)
    _, norm_back_in = jax.vjp(norm_rows, x_own32, gain_in)
    input_part, gain_one = norm_back_in(normed_in_grad)
    input_grad = resid_grad + input_part
    grad_qkv = mm_tn(normed_in, d_qkv).reshape(n_seq, n_fsdp, shard, 3 * cols)
    grad_qkv = lax.psum_scatter(grad_qkv, "fsdp", scatter_dimension=1, tiled=False)
    grad_qkv = lax.all_to_all(grad_qkv, "seq", split_axis=0, concat_axis=0, tiled=True)
    grad_qkv = (
        grad_qkv.reshape(n_seq, shard, 3, cols).transpose(2, 1, 0, 3).reshape(3, shard, width)
    )
    gains = lax.psum_scatter(
        jnp.stack([gain_one, gain_two]).reshape(2, n_dev, shard),
        AXES,
        scatter_dimension=1,
        tiled=False,
    )
    return (
        block_out[None],
        input_grad[None],
        gains[0],
        grad_qkv[0],
        grad_qkv[1],
        grad_qkv[2],
        grad_output,
        gains[1],
        grad_router,
        gate_weight_grad,
        up_weight_grad,
        down_grad,
    )


def solution(mesh):
    rows3 = P("fsdp", "seq", None)
    flat = P(AXES)
    two = P(AXES, None)
    three = P(AXES, None, None)
    return jax.shard_map(
        body,
        mesh=mesh,
        in_specs=(rows3, rows3, rows3, flat, two, two, two, two, flat, two, three, three, three),
        out_specs=(rows3, rows3, flat, two, two, two, two, flat, two, three, three, three),
        check_vma=False,
    )
```

profile of v0, /device:TPU:0, one launch (start us, length us, event | category | flops | bytes accessed | tf_op | source)
XLA Modules:
  0.0 1324.9 jit_solution(16863959521056442889)
XLA Ops:
  12.9 30.4 %all_to_all.34 = bf16[8,64,896]{2,1,0:T(8,128)(2,1)S(1)} all-to-all(bf16[8,64,896]{2,1,0:T(8,128)(2,1)S(1)} %copy.233), channel_id=1, replica_groups=mesh['seq'=8,'fsdp'=4] {'seq'}, dimensions={0} | all-to-all | bytes 1835008 | tf_op jit(solution)/shard_map/all_to_all | solution.py:120
  50.0 25.2 %all-gather.19.cloned.1.call-done = bf16[8,256,896]{2,0,1:T(8,128)(2,1)} async-done(((bf16[8,64,896]{2,0,1:T(8,128)(2,1)}), bf16[8,256,896]{2,0,1:T(8,128)(2,1)}) %all-gather.19.cloned.1.call-update) | async-done | bytes 3670032 | tf_op jit(solution)/shard_map/all_gather | solution.py:121
  80.2 69.8 %all-gather.17.cloned.1.call-done = bf16[1,1024,2048]{2,1,0:T(8,128)(2,1)} async-done(((bf16[1,128,2048]{2,1,0:T(8,128)(2,1)}), bf16[1,1024,2048]{2,1,0:T(8,128)(2,1)}) %all-gather.17.cloned.1.call-update) | async-done | bytes 4194320 | tf_op jit(solution)/shard_map/all_gather | solution.py:101
  174.6 9.4 fusion.8
  189.1 28.2 %all_to_all.35 = bf16[8,128,256]{1,2,0:T(8,128)(2,1)S(1)} all-to-all(bf16[8,128,256]{1,2,0:T(8,128)(2,1)S(1)} %copy.241), channel_id=1, replica_groups=mesh['seq'=8,'fsdp'=4] {'seq'}, dimensions={0} | all-to-all | bytes 1048576 | tf_op jit(solution)/shard_map/all_to_all | solution.py:143
  217.3 14.1 %all-gather.11.cloned.1.call-done = bf16[2048,2048]{1,0:T(8,128)(2,1)} async-done(((bf16[64,2048]{1,0:T(8,128)(2,1)}), bf16[2048,2048]{1,0:T(8,128)(2,1)}) %all-gather.11.cloned.1.call-update) | async-done | bytes 8388624 | tf_op jit(solution)/shard_map/all_gather | solution.py:126
  238.2 40.8 %all-gather.2 = s32[1,4096,8]{1,2,0:T(8,128)S(1)} all-gather(s32[1,128,8]{1,2,0:T(8,128)S(1)} %copy-done.24), channel_id=4, replica_groups=mesh['seq'=8,'fsdp'=4] {'seq','fsdp'}, dimensions={1}, use_global_device_ids=true | all-gather | bytes 135168 | tf_op jit(solution)/shard_map/all_gather | solution.py:100
  279.3 68.4 %all-gather.21.cloned.1.call-done = bf16[1,4096,2048]{2,1,0:T(8,128)(2,1)} async-done(((bf16[1,128,2048]{2,1,0:T(8,128)(2,1)}), bf16[1,4096,2048]{2,1,0:T(8,128)(2,1)}) %all-gather.21.cloned.1.call-update) | async-done | bytes 16777232 | tf_op jit(solution)/shard_map/all_gather | solution.py:128
  361.0 102.1 %all-gather.13.cloned.1.call-done = bf16[4096,2048]{1,0:T(8,128)(2,1)} async-done(((bf16[128,2048]{1,0:T(8,128)(2,1)}), bf16[4096,2048]{1,0:T(8,128)(2,1)}) %all-gather.13.cloned.1.call-update) | async-done | bytes 16777232 | tf_op jit(solution)/shard_map/all_gather | solution.py:147
  480.7 15.8 %fusion.98 = f32[2,1024,2,512]{3,1,2,0:T(8,128)} fusion(bf16[2,1024,2048,1]{2,1,3,0:T(8,128)(2,1)} %bitcast.248, bf16[2,2,2048,512]{3,2,1,0:T(8,128)(2,1)} %bitcast.297), kind=kOutput, calls=%fused_computation.181 | convolution fusion | flops 8589934592 | bytes 25165824 | tf_op jit(solution)/shard_map/erd,epdf->eprf/dot_general | solution.py:62
  496.4 15.0 %fusion.17 = (bf16[2,2,1024,512]{3,2,1,0:T(8,128)(2,1)S(1)}, f32[2,1024,2,512]{3,1,2,0:T(8,128)}) fusion(f32[2,1024,2,512]{3,1,2,0:T(8,128)} %fusion.98, bf16[2,1024,2048,1]{2,1,3,0:T(8,128)(2,1)S(1)} %bitcast.251, bf16[2,2,2048,512]{3,2,1,0:T(8,128)(2,1)} %bitcast.299), kind=kOutput, calls=%fused_computation.31 | convolution fusion | flops 8602517504 | bytes 37748736 | tf_op jit(solution)/shard_map/erd,epdf->eprf/dot_general | solution.py:62
  511.4 19.9 %fusion.3 = (f32[2,1024]{1,0:T(2,128)S(1)}, f32[2,1024,2048,1]{2,1,3,0:T(8,128)}) fusion(f32[2,32,32,2048]{3,2,1,0:T(8,128)} %copy.247, bf16[2,2,1024,512]{3,2,1,0:T(8,128)(2,1)S(1)} %get-tuple-element.133, bf16[2,2,512,2048]{3,2,1,0:T(8,128)(2,1)} %bitcast.295), kind=kOutput, calls=%fused_computation.8 | convolution fusion | flops 8598321152 | bytes 46145536 | tf_op jit(solution)/shard_map/eprf,epfd->erd/dot_general | solution.py:62
  531.4 11.0 fusion.97
  545.6 17.0 %fusion.2 = (bf16[2,1024,2048]{2,1,0:T(8,128)(2,1)}, bf16[2,1024,2048]{2,1,0:T(8,128)(2,1)}) fusion(f32[2,32,32,2048]{3,2,1,0:T(8,128)} %copy.247, f32[2,1024]{1,0:T(2,128)S(1)} %mul.567, f32[2,1024,2048,1]{2,1,3,0:T(8,128)} %get-tuple-element.136), kind=kLoop, calls=%fused_computation.7 | loop fusion | flops 16777216 | bytes 50339840 | tf_op jit(solution)/shard_map/convert_element_type | solution.py:166
  562.6 18.9 %fusion.16 = (bf16[2,2,1024,512]{3,2,1,0:T(8,128)(2,1)}, bf16[2,2,1024,512]{3,2,1,0:T(8,128)(2,1)S(1)}) fusion(f32[2,1024,2,512]{3,1,2,0:T(8,128)} %fusion.98, f32[2,1024,2,512]{3,1,2,0:T(8,128)} %get-tuple-element.134, bf16[2,2,512,2048]{3,2,1,0:T(8,128)(2,1)} %bitcast.296, bf16[2,1024,2048]{2,1,0:T(8,128)(2,1)} %get-tuple-element.122), kind=kOutput, calls=%fused_computation.29 | convolution fusion | flops 8617197568 | bytes 41943040 | tf_op jit(solution)/shard_map/erd,epfd->eprf/dot_general | solution.py:62
  581.5 16.2 %fusion.99 = f32[2,1024,2048,1]{2,1,3,0:T(8,128)} fusion(bf16[2,2,1024,512]{3,2,1,0:T(8,128)(2,1)S(1)} %get-tuple-element.98, bf16[2,2,2048,512]{3,2,1,0:T(8,128)(2,1)} %bitcast.298), kind=kOutput, calls=%fused_computation.182 | convolution fusion | flops 8589934592 | bytes 29360128 | tf_op jit(solution)/shard_map/eprf,epdf->erd/dot_general | solution.py:62
  597.6 16.9 %fusion.1 = bf16[2,1024,2048]{2,1,0:T(8,128)(2,1)} fusion(f32[2,1024,2048,1]{2,1,3,0:T(8,128)} %fusion.99, bf16[2,2,1024,512]{3,2,1,0:T(8,128)(2,1)} %get-tuple-element.97, bf16[2,2,2048,512]{3,2,1,0:T(8,128)(2,1)} %bitcast.300), kind=kOutput, calls=%fused_computation.4 | convolution fusion | flops 8598323200 | bytes 37748736 | tf_op jit(solution)/shard_map/eprf,epdf->erd/dot_general | solution.py:62
  614.6 10.7 bitcast_convert_fusion
  630.7 11.0 all-to-all-done.2
  641.9 167.0 %reduce-scatter.8.cloned.1.call-done = bf16[128,2048]{1,0:T(8,128)(2,1)} async-done(((bf16[4096,2048]{1,0:T(8,128)(2,1)}), bf16[128,2048]{1,0:T(8,128)(2,1)}) %reduce-scatter.8.cloned.1.call-update) | async-done | bytes 524304 | tf_op jit(solution)/shard_map/reduce_scatter | solution.py:186
  812.1 74.1 %all-gather.15.cloned.1.call-done = bf16[1024,2048]{1,0:T(8,128)(2,1)} async-done(((bf16[128,2048]{1,0:T(8,128)(2,1)}), bf16[1024,2048]{1,0:T(8,128)(2,1)}) %all-gather.15.cloned.1.call-update) | async-done | bytes 4194320 | tf_op jit(solution)/shard_map/all_gather | solution.py:211
  924.5 11.1 bitcast_convert_fusion.1
  937.0 16.9 %fusion.101 = f32[2,2,512,2048]{3,2,1,0:T(8,128)} fusion(bf16[2,2,1024,512]{3,2,1,0:T(8,128)(2,1)} %copy-done.34, bf16[2,1024,2048,1]{2,1,3,0:T(8,128)(2,1)} %bitcast.249), kind=kOutput, calls=%fused_computation.184 | convolution fusion | flops 8589934592 | bytes 29360128 | tf_op jit(solution)/shard_map/erd,eprf->epdf/dot_general | solution.py:62
  956.6 16.5 %fusion.102 = f32[2,2,512,2048]{3,2,1,0:T(8,128)} fusion(bf16[2,2,1024,512]{3,2,1,0:T(8,128)(2,1)} %get-tuple-element.97, bf16[2,1024,2048,1]{2,1,3,0:T(8,128)(2,1)} %bitcast.250), kind=kOutput, calls=%fused_computation.185 | convolution fusion | flops 8589934592 | bytes 29360128 | tf_op jit(solution)/shard_map/erd,eprf->epdf/dot_general | solution.py:62
  979.7 16.6 %fusion.9 = f32[2,2,512,2048]{3,2,1,0:T(8,128)} fusion(bf16[2,2,1024,512]{3,2,1,0:T(8,128)(2,1)} %copy-done.33, bf16[2,1024,2048]{2,1,0:T(8,128)(2,1)} %get-tuple-element.122), kind=kOutput, calls=%fused_computation.20 | convolution fusion | flops 8589934592 | bytes 29360128 | tf_op jit(solution)/shard_map/eprf,erd->epfd/dot_general | solution.py:62
  996.3 16.4 %copy.269 = f32[4,2048,512]{2,1,0:T(8,128)} copy(f32[4,2048,512]{1,2,0:T(8,128)} %bitcast.240) | data formatting | bytes 33554432
  1012.6 16.5 %copy.270 = f32[4,2048,512]{2,1,0:T(8,128)} copy(f32[4,2048,512]{1,2,0:T(8,128)} %bitcast.241) | data formatting | bytes 33554432
  1029.1 42.9 %all_gather.35 = bf16[4096,64]{0,1:T(8,128)(2,1)S(1)} all-gather(bf16[128,64]{0,1:T(8,128)(2,1)S(1)} %multiply_convert_fusion.2), channel_id=1, replica_groups=mesh['seq'=8,'fsdp'=4] {'seq','fsdp'}, dimensions={0}, use_global_device_ids=true | all-gather | bytes 540672 | tf_op jit(solution)/shard_map/all_gather | solution.py:204
  1074.6 21.2 %reduce-scatter.10.cloned.1.call-done = bf16[128,2048]{1,0:T(8,128)(2,1)} async-done(((bf16[1024,2048]{1,0:T(8,128)(2,1)}), bf16[128,2048]{1,0:T(8,128)(2,1)}) %reduce-scatter.10.cloned.1.call-update) | async-done | bytes 524304 | tf_op jit(solution)/shard_map/reduce_scatter | solution.py:225
  1097.6 45.8 %all-reduce = f32[2,32,64]{2,0,1:T(2,128)S(1)} all-reduce(f32[2,32,64]{2,0,1:T(2,128)S(1)} %pad_maximum_fusion.7), channel_id=9, replica_groups=mesh['seq'=8,'fsdp'=4] {'seq','fsdp'}, use_global_device_ids=true, to_apply=%region_27.28.clone | all-reduce | flops 4096 | bytes 32768
  1144.0 138.5 %reduce-scatter.6.cloned.1.call-done = bf16[128,2048]{1,0:T(8,128)(2,1)} async-done(((bf16[4096,2048]{1,0:T(8,128)(2,1)}), bf16[128,2048]{1,0:T(8,128)(2,1)}) %reduce-scatter.6.cloned.1.call-update) | async-done | bytes 524304 | tf_op jit(solution)/shard_map/reduce_scatter | solution.py:195
  1293.2 25.0 %reduce-scatter.14.cloned.1.call-done = f32[64,2048]{1,0:T(8,128)} async-done(((f32[256,2048]{1,0:T(8,128)}), f32[64,2048]{1,0:T(8,128)}) %reduce-scatter.14.cloned.1.call-update) | async-done | bytes 524304 | tf_op jit(solution)/shard_map/reduce_scatter | solution.py:213
  (200 shorter events, 161.1 us)
Async XLA Ops:
  7.2 67.9 %all-gather.19.cloned.1.call-start = ((), (), s32[]{:S(2)}) async-start(), calls=%async_computation.18 | async-start | bytes 4587520 | tf_op jit(solution)/shard_map/all_gather | solution.py:121
  44.7 105.3 %all-gather.17.cloned.1.call-start = ((), (), s32[]{:S(2)}) async-start(), calls=%async_computation.17 | async-start | bytes 4718592 | tf_op jit(solution)/shard_map/all_gather | solution.py:101
  45.5 185.9 %all-gather.11.cloned.1.call-start = ((), (), s32[]{:S(2)}) async-start(), calls=%async_computation.9 | async-start | bytes 8650752 | tf_op jit(solution)/shard_map/all_gather | solution.py:126
  46.2 301.5 %all-gather.21.cloned.1.call-start = ((), (), s32[]{:S(2)}) async-start(), calls=%async_computation.19 | async-start | bytes 17301504 | tf_op jit(solution)/shard_map/all_gather | solution.py:128
  46.8 416.2 %all-gather.13.cloned.1.call-start = ((), (), s32[]{:S(2)}) async-start(), calls=%async_computation.10 | async-start | bytes 17301504 | tf_op jit(solution)/shard_map/all_gather | solution.py:147
  49.9 121.3 %copy-start.6 = (f32[1024,64]{1,0:T(8,128)}, f32[1024,64]{1,0:T(8,128)S(1)}, u32[]{:S(2)}) copy-start(f32[1024,64]{1,0:T(8,128)S(1)} %get-tuple-element.126) | copy-start | bytes 786436
  80.2 72.9 %copy-start.22 = (f32[2048]{0:T(1024)}, f32[2048]{0:T(1024)S(1)}, u32[]{:S(2)}) copy-start(f32[2048]{0:T(1024)S(1)} %get-tuple-element.85) | copy-start | bytes 24580
  80.2 156.0 %copy-start.20 = (f32[2048]{0:T(1024)}, f32[2048]{0:T(1024)S(1)}, u32[]{:S(2)}) copy-start(f32[2048]{0:T(1024)S(1)} %get-tuple-element.84) | copy-start | bytes 24580
  160.4 23.6 %copy-start.10 = (bf16[1024,256]{0,1:T(8,128)(2,1)}, bf16[1024,256]{0,1:T(8,128)(2,1)S(1)}, u32[]{:S(2)}) copy-start(bf16[1024,256]{0,1:T(8,128)(2,1)S(1)} %slice.127) | copy-start | bytes 1572868
  184.0 47.4 %copy-start.2 = (bf16[1,128,2048]{2,1,0:T(8,128)(2,1)S(1)}, bf16[1,128,2048]{2,1,0:T(8,128)(2,1)}, u32[]{:S(2)}) copy-start(bf16[1,128,2048]{2,1,0:T(8,128)(2,1)} %param.13) | copy-start | bytes 1572868
  236.2 42.8 %copy-start.30 = (f32[128]{0:T(128)}, f32[128]{0:T(128)S(1)}, u32[]{:S(2)}) copy-start(f32[128]{0:T(128)S(1)} %get-tuple-element.129) | copy-start | bytes 1540
  236.2 42.8 %copy-start.26 = (f32[128]{0:T(128)}, f32[128]{0:T(128)S(1)}, u32[]{:S(2)}) copy-start(f32[128]{0:T(128)S(1)} %fusion.86) | copy-start | bytes 1540
  238.1 570.7 %reduce-scatter.8.cloned.1.call-start = ((), (), s32[]{:S(2)}) async-start(), calls=%async_computation.12 | async-start | bytes 17301504 | tf_op jit(solution)/shard_map/reduce_scatter | solution.py:186
  480.7 15.8 %copy-start.5 = (bf16[2,32,32,2048]{3,2,1,0:T(8,128)(2,1)S(1)}, bf16[2,32,32,2048]{3,2,1,0:T(8,128)(2,1)}, u32[]{:S(2)}) copy-start(bf16[2,32,32,2048]{3,2,1,0:T(8,128)(2,1)} %copy.245) | copy-start | bytes 25165828
  511.4 19.9 %copy-start.33 = (bf16[2,2,1024,512]{3,2,1,0:T(8,128)(2,1)}, bf16[2,2,1024,512]{3,2,1,0:T(8,128)(2,1)S(1)}, u32[]{:S(2)}) copy-start(bf16[2,2,1024,512]{3,2,1,0:T(8,128)(2,1)S(1)} %get-tuple-element.133) | copy-start | bytes 12582916
  581.5 16.2 %copy-start.34 = (bf16[2,2,1024,512]{3,2,1,0:T(8,128)(2,1)}, bf16[2,2,1024,512]{3,2,1,0:T(8,128)(2,1)S(1)}, u32[]{:S(2)}) copy-start(bf16[2,2,1024,512]{3,2,1,0:T(8,128)(2,1)S(1)} %get-tuple-element.98) | copy-start | bytes 12582916
  625.3 16.3 %copy-start.25 = (s32[1,128,8]{1,2,0:T(8,128)S(1)}, s32[1,128,8]{1,2,0:T(8,128)}, u32[]{:S(2)}) copy-start(s32[1,128,8]{1,2,0:T(8,128)} %param.15) | copy-start | bytes 12292
  625.3 183.5 %copy-start.1 = (f32[128,2048]{1,0:T(8,128)S(1)}, f32[128,2048]{1,0:T(8,128)}, u32[]{:S(2)}) copy-start(f32[128,2048]{1,0:T(8,128)} %copy-done) | copy-start | bytes 3145732
  625.3 183.5 %copy-start.21 = (f32[2048]{0:T(1024)S(1)}, f32[2048]{0:T(1024)}, u32[]{:S(2)}) copy-start(f32[2048]{0:T(1024)} %copy-done.20) | copy-start | bytes 24580
  625.3 183.5 %copy-start.27 = (f32[128]{0:T(128)S(1)}, f32[128]{0:T(128)}, u32[]{:S(2)}) copy-start(f32[128]{0:T(128)} %copy-done.26) | copy-start | bytes 1540
  625.3 185.3 %copy-start.31 = (f32[128]{0:T(128)S(1)}, f32[128]{0:T(128)}, u32[]{:S(2)}) copy-start(f32[128]{0:T(128)} %copy-done.30) | copy-start | bytes 1540
  625.4 185.3 %copy-start.9 = (bf16[1,128,2048]{2,1,0:T(8,128)(2,1)S(1)}, bf16[1,128,2048]{2,1,0:T(8,128)(2,1)}, u32[]{:S(2)}) copy-start(bf16[1,128,2048]{2,1,0:T(8,128)(2,1)} %param.14) | copy-start | bytes 1572868
  627.8 13.9 %all-to-all-start.2 = ((f32[32,2,128]{2,1,0:T(2,128)}), f32[32,2,128]{2,1,0:T(2,128)S(1)}, u32[]{:S(2)}, u32[]{:S(2)}) async-start(f32[32,2,128]{2,1,0:T(2,128)} %get-tuple-element.92), calls=%async_computation.4 | async-start | bytes 65536 | tf_op jit(solution)/shard_map/all_to_all | solution.py:191
  630.6 255.6 %all-gather.15.cloned.1.call-start = ((), (), s32[]{:S(2)}) async-start(), calls=%async_computation.13 | async-start | bytes 4718592 | tf_op jit(solution)/shard_map/all_gather | solution.py:211
  811.9 162.1 %reduce-scatter.12.cloned.1.call-start = ((), (), s32[]{:S(2)}) async-start(), calls=%async_computation.15 | async-start | bytes 7864320 | tf_op jit(solution)/shard_map/reduce_scatter | solution.py:230
  812.1 84.1 %copy-start.11 = (bf16[1024,256]{0,1:T(8,128)(2,1)S(1)}, bf16[1024,256]{0,1:T(8,128)(2,1)}, u32[]{:S(2)}) copy-start(bf16[1024,256]{0,1:T(8,128)(2,1)} %copy-done.10) | copy-start | bytes 1572868
  916.4 179.5 %reduce-scatter.10.cloned.1.call-start = ((), (), s32[]{:S(2)}) async-start(), calls=%async_computation.14 | async-start | bytes 4718592 | tf_op jit(solution)/shard_map/reduce_scatter | solution.py:225
  924.5 358.0 %reduce-scatter.6.cloned.1.call-start = ((), (), s32[]{:S(2)}) async-start(), calls=%async_computation.11 | async-start | bytes 17301504 | tf_op jit(solution)/shard_map/reduce_scatter | solution.py:195
  935.6 382.6 %reduce-scatter.14.cloned.1.call-start = ((), (), s32[]{:S(2)}) async-start(), calls=%async_computation.16 | async-start | bytes 2621440 | tf_op jit(solution)/shard_map/reduce_scatter | solution.py:213
  937.0 17.0 %copy-start.18 = (bf16[2,128,1024]{2,1,0:T(8,128)(2,1)S(1)}, bf16[2,128,1024]{2,1,0:T(8,128)(2,1)}, u32[]{:S(2)}) copy-start(bf16[2,128,1024]{2,1,0:T(8,128)(2,1)} %copy-done.17) | copy-start | bytes 1572868
  937.0 17.0 %copy-start.32 = (bf16[1024,2048]{1,0:T(8,128)(2,1)S(1)}, bf16[1024,2048]{1,0:T(8,128)(2,1)}, u32[]{:S(2)}) copy-start(bf16[1024,2048]{1,0:T(8,128)(2,1)} %all-gather.15.cloned.1.call-done) | copy-start | bytes 12582916
  973.9 311.4 %all-to-all-start.3 = ((f32[8,64,768]{2,1,0:T(8,128)}), f32[8,64,768]{2,1,0:T(8,128)}, u32[]{:S(2)}, u32[]{:S(2)}) async-start(f32[8,64,768]{2,1,0:T(8,128)} %bitcast.270), calls=%async_computation.7 | async-start | bytes 3145728 | tf_op jit(solution)/shard_map/all_to_all | solution.py:231
  (18 other events, 62.0 us)
Sparse Core Ops, SparseCore 0:
  44.9 30.1 all-gather.18
  77.2 72.7 all-gather.16
  152.9 78.4 all-gather.10
  234.1 113.5 all-gather.20
  350.5 112.5 all-gather.12
  625.5 183.2 reduce-scatter.7
  812.0 74.2 all-gather.14
  916.5 57.3 reduce-scatter.11
  977.6 118.2 reduce-scatter.9
  1098.0 184.4 reduce-scatter.5
  1285.6 32.5 reduce-scatter.13
where the time goes:
time: 1340 us; the launch traced here: 1320 us
  waiting for transfers between devices  719 us (54%)
  matrix products  265 us (20%)
  blocking collectives  188 us (14%)
  local copies, waits for them, and re-layouts  88.1 us (7%)
  other arithmetic  40.5 us (3%)
  between operations  14.8 us (1%)
    dot_general x19, matrix products, ein(): return jnp.einsum(spec, *args, preferred_element_type=f32)  206 us
    reduce_scatter x1, waiting for transfers between devices, body(): lax.psum_scatter(spread(back), AXES, scatter_dimension=0, tiled=True)  167 us
    reduce_scatter x1, waiting for transfers between devices, body(): lax.psum_scatter(spread(w_rows * out), AXES, scatter_dimension=0, tiled=T...  139 us
    all_gather x1, waiting for transfers between devices, body(): x_all = lax.all_gather(normed_mid, AXES, axis=0, tiled=True)  102 us
    all_gather x1, waiting for transfers between devices, body(): lax.all_gather(resid_grad.astype(bf16), 'seq', axis=0, tiled=True)  74.1 us
    all_gather x1, waiting for transfers between devices, body(): x_seq = lax.all_gather(x_own, 'seq', axis=0, tiled=True)  69.8 us
    all_gather x1, waiting for transfers between devices, body(): cot_all = lax.all_gather(cot_own, AXES, axis=0, tiled=True)  68.4 us
    unnamed x88, local copies, waits for them, and re-layouts  51 us
  transfers between devices with their start and end apart: 13, of which 12 were waited for; matrix products, arithmetic and copies ran while one was open for 14% of the time, Pallas kernels for 0%

commit v1 on v0

--- a/solution.py
+++ b/solution.py
@@ -98,7 +98,14 @@
     cot_own = cotangent[0]
     chosen = routes[0]
     routes_all = lax.all_gather(chosen, AXES, axis=0, tiled=True)
-    x_seq = lax.all_gather(x_own, "seq", axis=0, tiled=True)
+    n_dev_2 = lax.axis_size("seq")
+    route = [(i, (i + 1) % n_dev_2) for i in range(n_dev_2)]
+    parts = [x_own]
+    for stride in range(1, n_dev_2):
+        parts = [lax.ppermute(parts[0], "seq", route), *parts]
+    result = jnp.concatenate(parts, axis=0)
+    shift = (lax.axis_index("seq") + 1) * parts[-1].shape[0]
+    x_seq = jnp.roll(result, shift, axis=0)
     small = jnp.concatenate(
         [
             router_weight,

time: 1340 us -> 1280 us (0.955); the launches traced: 1320 us -> 1280 us
  waiting for transfers between devices: 719 us -> 669 us
    ppermute x0 -> x7, waiting for transfers between devices: none -> 115 us  [body(): parts = [lax.ppermute(parts[0], 'seq', route), *parts]]
    all_gather x1 -> x0, waiting for transfers between devices: 69.8 us -> none  [body(): x_seq = lax.all_gather(x_own, 'seq', axis=0, tiled=True)]
    all_gather x1, waiting for transfers between devices: 68.4 us -> 12.5 us  [body(): cot_all = lax.all_gather(cot_own, AXES, axis=0, tiled=True)]
    all_gather x1, waiting for transfers between devices: 25.2 us -> 0.02 us  [body(): lax.all_gather(moved, 'fsdp', axis=1).reshape(width, 3 * cols + 128)]
    all_gather x1, waiting for transfers between devices: 14.1 us -> 0.01 us  [body(): out_full = lax.all_gather(output_weight, AXES, axis=0, tiled=True)]
    unnamed x88 -> x113, local copies, waits for them, and re-layouts: 51 us -> 60.4 us
  transfers between devices with their start and end apart: 13 -> 19, of which waited for: 12 -> 16; matrix products, arithmetic and copies ran while one was open for 14% -> 15% of each run, Pallas kernels for 0% -> 0%
where the time goes in v1:
time: 1280 us
  waiting for transfers between devices  669 us (52%)
  matrix products  262 us (20%)
  blocking collectives  187 us (15%)
  local copies, waits for them, and re-layouts  97.5 us (8%)
  other arithmetic  38.6 us (3%)
  between operations  15.3 us (1%)
    dot_general x19, matrix products, ein(): return jnp.einsum(spec, *args, preferred_element_type=f32)  206 us
    reduce_scatter x1, waiting for transfers between devices, body(): lax.psum_scatter(spread(back), AXES, scatter_dimension=0, tiled=True)  166 us
    reduce_scatter x1, waiting for transfers between devices, body(): lax.psum_scatter(spread(w_rows * out), AXES, scatter_dimension=0, tiled=T...  140 us
    ppermute x7, waiting for transfers between devices, body(): parts = [lax.ppermute(parts[0], 'seq', route), *parts]  115 us
    all_gather x1, waiting for transfers between devices, body(): x_all = lax.all_gather(normed_mid, AXES, axis=0, tiled=True)  102 us
    all_gather x1, waiting for transfers between devices, body(): lax.all_gather(resid_grad.astype(bf16), 'seq', axis=0, tiled=True)  74 us
    unnamed x113, local copies, waits for them, and re-layouts  60.4 us
    unnamed x1, blocking collectives  44.9 us
  transfers between devices with their start and end apart: 19, of which 16 were waited for; matrix products, arithmetic and copies ran while one was open for 15% of the time, Pallas kernels for 0%

profile of v1, /device:TPU:0, one launch (start us, length us, event | category | flops | bytes accessed | tf_op | source)
XLA Modules:
  0.0 1279.2 jit_solution(1104102438059182578)
XLA Ops:
  13.0 30.4 %all_to_all.34 = bf16[8,64,896]{2,1,0:T(8,128)(2,1)S(1)} all-to-all(bf16[8,64,896]{2,1,0:T(8,128)(2,1)S(1)} %copy.233), channel_id=1, replica_groups=mesh['seq'=8,'fsdp'=4] {'seq'}, dimensions={0} | all-to-all | bytes 1835008 | tf_op jit(solution)/shard_map/all_to_all | solution.py:127
  47.5 13.7 %collective-permute-done = bf16[128,2048]{1,0:T(8,128)(2,1)S(1)} collective-permute-done((bf16[128,2048]{1,0:T(8,128)(2,1)S(1)}, bf16[128,2048]{1,0:T(8,128)(2,1)S(1)}, u32[]{:S(2)}, u32[]{:S(2)}) %collective-permute-start) | collective-permute-done | bytes 524320 | tf_op jit(solution)/shard_map/ppermute | solution.py:105
  61.2 13.9 %collective-permute-done.1 = bf16[128,2048]{1,0:T(8,128)(2,1)S(1)} collective-permute-done((bf16[128,2048]{1,0:T(8,128)(2,1)S(1)}, bf16[128,2048]{1,0:T(8,128)(2,1)S(1)}, u32[]{:S(2)}, u32[]{:S(2)}) %collective-permute-start.1) | collective-permute-done | bytes 524320 | tf_op jit(solution)/shard_map/ppermute | solution.py:105
  75.1 13.0 %collective-permute-done.2 = bf16[128,2048]{1,0:T(8,128)(2,1)S(1)} collective-permute-done((bf16[128,2048]{1,0:T(8,128)(2,1)S(1)}, bf16[128,2048]{1,0:T(8,128)(2,1)S(1)}, u32[]{:S(2)}, u32[]{:S(2)}) %collective-permute-start.2) | collective-permute-done | bytes 524320 | tf_op jit(solution)/shard_map/ppermute | solution.py:105
  88.1 17.8 %collective-permute-done.3 = bf16[128,2048]{1,0:T(8,128)(2,1)S(1)} collective-permute-done((bf16[128,2048]{1,0:T(8,128)(2,1)S(1)}, bf16[128,2048]{1,0:T(8,128)(2,1)S(1)}, u32[]{:S(2)}, u32[]{:S(2)}) %collective-permute-start.3) | collective-permute-done | bytes 524320 | tf_op jit(solution)/shard_map/ppermute | solution.py:105
  105.9 22.3 %collective-permute-done.4 = bf16[128,2048]{1,0:T(8,128)(2,1)S(1)} collective-permute-done((bf16[128,2048]{1,0:T(8,128)(2,1)S(1)}, bf16[128,2048]{1,0:T(8,128)(2,1)S(1)}, u32[]{:S(2)}, u32[]{:S(2)}) %collective-permute-start.4) | collective-permute-done | bytes 524320 | tf_op jit(solution)/shard_map/ppermute | solution.py:105
  128.2 12.1 collective-permute-done.5
  143.7 21.9 %collective-permute-done.6 = bf16[128,2048]{1,0:T(8,128)(2,1)} collective-permute-done((bf16[128,2048]{1,0:T(8,128)(2,1)}, bf16[128,2048]{1,0:T(8,128)(2,1)}, u32[]{:S(2)}, u32[]{:S(2)}) %collective-permute-start.6) | collective-permute-done | bytes 524320 | tf_op jit(solution)/shard_map/ppermute | solution.py:105
  214.3 25.3 %all_to_all.35 = bf16[8,128,256]{1,2,0:T(8,128)(2,1)S(1)} all-to-all(bf16[8,128,256]{1,2,0:T(8,128)(2,1)S(1)} %copy.241), channel_id=1, replica_groups=mesh['seq'=8,'fsdp'=4] {'seq'}, dimensions={0} | all-to-all | bytes 1048576 | tf_op jit(solution)/shard_map/all_to_all | solution.py:150
  246.3 43.5 %all-gather.1 = s32[1,4096,8]{1,2,0:T(8,128)S(1)} all-gather(s32[1,128,8]{1,2,0:T(8,128)S(1)} %copy-done.29), channel_id=3, replica_groups=mesh['seq'=8,'fsdp'=4] {'seq','fsdp'}, dimensions={1}, use_global_device_ids=true | all-gather | bytes 135168 | tf_op jit(solution)/shard_map/all_gather | solution.py:100
  290.1 12.5 all-gather.17.cloned.1.call-done
  315.9 102.1 %all-gather.11.cloned.1.call-done = bf16[4096,2048]{1,0:T(8,128)(2,1)} async-done(((bf16[128,2048]{1,0:T(8,128)(2,1)}), bf16[4096,2048]{1,0:T(8,128)(2,1)}) %all-gather.11.cloned.1.call-update) | async-done | bytes 16777232 | tf_op jit(solution)/shard_map/all_gather | solution.py:154
  435.6 15.8 %fusion.100 = f32[2,1024,2,512]{3,1,2,0:T(8,128)} fusion(bf16[2,1024,2048,1]{2,1,3,0:T(8,128)(2,1)} %bitcast.244, bf16[2,2,2048,512]{3,2,1,0:T(8,128)(2,1)} %bitcast.293), kind=kOutput, calls=%fused_computation.199 | convolution fusion | flops 8589934592 | bytes 25165824 | tf_op jit(solution)/shard_map/erd,epdf->eprf/dot_general | solution.py:62
  451.4 15.0 %fusion.17 = (bf16[2,2,1024,512]{3,2,1,0:T(8,128)(2,1)S(1)}, f32[2,1024,2,512]{3,1,2,0:T(8,128)}) fusion(f32[2,1024,2,512]{3,1,2,0:T(8,128)} %fusion.100, bf16[2,1024,2048,1]{2,1,3,0:T(8,128)(2,1)S(1)} %bitcast.247, bf16[2,2,2048,512]{3,2,1,0:T(8,128)(2,1)} %bitcast.295), kind=kOutput, calls=%fused_computation.31 | convolution fusion | flops 8602517504 | bytes 37748736 | tf_op jit(solution)/shard_map/erd,epdf->eprf/dot_general | solution.py:62
  466.3 19.9 %fusion.3 = (f32[2,1024]{1,0:T(2,128)S(1)}, f32[2,1024,2048,1]{2,1,3,0:T(8,128)}) fusion(f32[2,32,32,2048]{3,2,1,0:T(8,128)} %copy.247, bf16[2,2,1024,512]{3,2,1,0:T(8,128)(2,1)S(1)} %get-tuple-element.133, bf16[2,2,512,2048]{3,2,1,0:T(8,128)(2,1)} %bitcast.291), kind=kOutput, calls=%fused_computation.8 | convolution fusion | flops 8598321152 | bytes 46145536 | tf_op jit(solution)/shard_map/eprf,epfd->erd/dot_general | solution.py:62
  500.5 17.0 %fusion.2 = (bf16[2,1024,2048]{2,1,0:T(8,128)(2,1)}, bf16[2,1024,2048]{2,1,0:T(8,128)(2,1)}) fusion(f32[2,32,32,2048]{3,2,1,0:T(8,128)} %copy.247, f32[2,1024]{1,0:T(2,128)S(1)} %mul.571, f32[2,1024,2048,1]{2,1,3,0:T(8,128)} %get-tuple-element.136), kind=kLoop, calls=%fused_computation.7 | loop fusion | flops 16777216 | bytes 50339840 | tf_op jit(solution)/shard_map/convert_element_type | solution.py:173
  517.5 18.7 %fusion.16 = (bf16[2,2,1024,512]{3,2,1,0:T(8,128)(2,1)}, bf16[2,2,1024,512]{3,2,1,0:T(8,128)(2,1)S(1)}) fusion(f32[2,1024,2,512]{3,1,2,0:T(8,128)} %fusion.100, f32[2,1024,2,512]{3,1,2,0:T(8,128)} %get-tuple-element.134, bf16[2,2,512,2048]{3,2,1,0:T(8,128)(2,1)} %bitcast.292, bf16[2,1024,2048]{2,1,0:T(8,128)(2,1)} %get-tuple-element.122), kind=kOutput, calls=%fused_computation.29 | convolution fusion | flops 8617197568 | bytes 41943040 | tf_op jit(solution)/shard_map/erd,epfd->eprf/dot_general | solution.py:62
  536.2 16.2 %fusion.101 = f32[2,1024,2048,1]{2,1,3,0:T(8,128)} fusion(bf16[2,2,1024,512]{3,2,1,0:T(8,128)(2,1)S(1)} %get-tuple-element.98, bf16[2,2,2048,512]{3,2,1,0:T(8,128)(2,1)} %bitcast.294), kind=kOutput, calls=%fused_computation.200 | convolution fusion | flops 8589934592 | bytes 29360128 | tf_op jit(solution)/shard_map/eprf,epdf->erd/dot_general | solution.py:62
  552.4 16.9 %fusion.1 = bf16[2,1024,2048]{2,1,0:T(8,128)(2,1)} fusion(f32[2,1024,2048,1]{2,1,3,0:T(8,128)} %fusion.101, bf16[2,2,1024,512]{3,2,1,0:T(8,128)(2,1)} %get-tuple-element.97, bf16[2,2,2048,512]{3,2,1,0:T(8,128)(2,1)} %bitcast.296), kind=kOutput, calls=%fused_computation.4 | convolution fusion | flops 8598323200 | bytes 37748736 | tf_op jit(solution)/shard_map/eprf,epdf->erd/dot_general | solution.py:62
  596.6 166.1 %reduce-scatter.8.cloned.1.call-done = bf16[128,2048]{1,0:T(8,128)(2,1)} async-done(((bf16[4096,2048]{1,0:T(8,128)(2,1)}), bf16[128,2048]{1,0:T(8,128)(2,1)}) %reduce-scatter.8.cloned.1.call-update) | async-done | bytes 524304 | tf_op jit(solution)/shard_map/reduce_scatter | solution.py:193
  765.9 74.0 %all-gather.13.cloned.1.call-done = bf16[1024,2048]{1,0:T(8,128)(2,1)} async-done(((bf16[128,2048]{1,0:T(8,128)(2,1)}), bf16[1024,2048]{1,0:T(8,128)(2,1)}) %all-gather.13.cloned.1.call-update) | async-done | bytes 4194320 | tf_op jit(solution)/shard_map/all_gather | solution.py:218
  878.4 11.1 bitcast_convert_fusion.1
  891.0 16.9 %fusion.103 = f32[2,2,512,2048]{3,2,1,0:T(8,128)} fusion(bf16[2,2,1024,512]{3,2,1,0:T(8,128)(2,1)} %copy-done.39, bf16[2,1024,2048,1]{2,1,3,0:T(8,128)(2,1)} %bitcast.245), kind=kOutput, calls=%fused_computation.202 | convolution fusion | flops 8589934592 | bytes 29360128 | tf_op jit(solution)/shard_map/erd,eprf->epdf/dot_general | solution.py:62
  910.5 16.5 %fusion.104 = f32[2,2,512,2048]{3,2,1,0:T(8,128)} fusion(bf16[2,2,1024,512]{3,2,1,0:T(8,128)(2,1)} %get-tuple-element.97, bf16[2,1024,2048,1]{2,1,3,0:T(8,128)(2,1)} %bitcast.246), kind=kOutput, calls=%fused_computation.203 | convolution fusion | flops 8589934592 | bytes 29360128 | tf_op jit(solution)/shard_map/erd,eprf->epdf/dot_general | solution.py:62
  933.6 16.6 %fusion.9 = f32[2,2,512,2048]{3,2,1,0:T(8,128)} fusion(bf16[2,2,1024,512]{3,2,1,0:T(8,128)(2,1)} %copy-done.38, bf16[2,1024,2048]{2,1,0:T(8,128)(2,1)} %get-tuple-element.122), kind=kOutput, calls=%fused_computation.20 | convolution fusion | flops 8589934592 | bytes 29360128 | tf_op jit(solution)/shard_map/eprf,erd->epfd/dot_general | solution.py:62
  950.2 16.3 %copy.269 = f32[4,2048,512]{2,1,0:T(8,128)} copy(f32[4,2048,512]{1,2,0:T(8,128)} %bitcast.236) | data formatting | bytes 33554432
  966.6 16.4 %copy.270 = f32[4,2048,512]{2,1,0:T(8,128)} copy(f32[4,2048,512]{1,2,0:T(8,128)} %bitcast.237) | data formatting | bytes 33554432
  983.0 42.8 %all_gather.31 = bf16[4096,64]{0,1:T(8,128)(2,1)S(1)} all-gather(bf16[128,64]{0,1:T(8,128)(2,1)S(1)} %multiply_convert_fusion.2), channel_id=1, replica_groups=mesh['seq'=8,'fsdp'=4] {'seq','fsdp'}, dimensions={0}, use_global_device_ids=true | all-gather | bytes 540672 | tf_op jit(solution)/shard_map/all_gather | solution.py:211
  1028.4 21.4 %reduce-scatter.10.cloned.1.call-done = bf16[128,2048]{1,0:T(8,128)(2,1)} async-done(((bf16[1024,2048]{1,0:T(8,128)(2,1)}), bf16[128,2048]{1,0:T(8,128)(2,1)}) %reduce-scatter.10.cloned.1.call-update) | async-done | bytes 524304 | tf_op jit(solution)/shard_map/reduce_scatter | solution.py:232
  1051.6 44.9 %all-reduce = f32[2,32,64]{2,0,1:T(2,128)S(1)} all-reduce(f32[2,32,64]{2,0,1:T(2,128)S(1)} %pad_maximum_fusion.7), channel_id=8, replica_groups=mesh['seq'=8,'fsdp'=4] {'seq','fsdp'}, use_global_device_ids=true, to_apply=%region_27.28.clone | all-reduce | flops 4096 | bytes 32768
  1097.0 140.3 %reduce-scatter.6.cloned.1.call-done = bf16[128,2048]{1,0:T(8,128)(2,1)} async-done(((bf16[4096,2048]{1,0:T(8,128)(2,1)}), bf16[128,2048]{1,0:T(8,128)(2,1)}) %reduce-scatter.6.cloned.1.call-update) | async-done | bytes 524304 | tf_op jit(solution)/shard_map/reduce_scatter | solution.py:202
  1248.0 24.1 %reduce-scatter.14.cloned.1.call-done = f32[64,2048]{1,0:T(8,128)} async-done(((f32[256,2048]{1,0:T(8,128)}), f32[64,2048]{1,0:T(8,128)}) %reduce-scatter.14.cloned.1.call-update) | async-done | bytes 524304 | tf_op jit(solution)/shard_map/reduce_scatter | solution.py:220
  (237 shorter events, 208.7 us)
Async XLA Ops:
  7.2 39.2 %copy-start.2 = (bf16[1,128,2048]{2,1,0:T(8,128)(2,1)S(1)}, bf16[1,128,2048]{2,1,0:T(8,128)(2,1)}, u32[]{:S(2)}) copy-start(bf16[1,128,2048]{2,1,0:T(8,128)(2,1)} %param.13) | copy-start | bytes 1572868
  7.2 168.8 %all-gather.15.cloned.1.call-start = ((), (), s32[]{:S(2)}) async-start(), calls=%async_computation.17 | async-start | bytes 4587520 | tf_op jit(solution)/shard_map/all_gather | solution.py:128
  44.8 194.7 %all-gather.9.cloned.1.call-start = ((), (), s32[]{:S(2)}) async-start(), calls=%async_computation.9 | async-start | bytes 8650752 | tf_op jit(solution)/shard_map/all_gather | solution.py:133
  45.6 257.1 %all-gather.17.cloned.1.call-start = ((), (), s32[]{:S(2)}) async-start(), calls=%async_computation.18 | async-start | bytes 17301504 | tf_op jit(solution)/shard_map/all_gather | solution.py:135
  46.3 371.7 %all-gather.11.cloned.1.call-start = ((), (), s32[]{:S(2)}) async-start(), calls=%async_computation.10 | async-start | bytes 17301504 | tf_op jit(solution)/shard_map/all_gather | solution.py:154
  46.4 14.8 %collective-permute-start = (bf16[128,2048]{1,0:T(8,128)(2,1)S(1)}, bf16[128,2048]{1,0:T(8,128)(2,1)S(1)}, u32[]{:S(2)}, u32[]{:S(2)}) collective-permute-start(bf16[128,2048]{1,0:T(8,128)(2,1)S(1)} %bitcast.235), channel_id=1, source_target_pairs={{0,4},{4,8},{8,12},{12,16},{16,20},{20,24},{24,28},{28,0},{1,5},{5... | collective-permute-start | bytes 1572872 | tf_op jit(solution)/shard_map/ppermute | solution.py:105
  61.2 13.9 %collective-permute-start.1 = (bf16[128,2048]{1,0:T(8,128)(2,1)S(1)}, bf16[128,2048]{1,0:T(8,128)(2,1)S(1)}, u32[]{:S(2)}, u32[]{:S(2)}) collective-permute-start(bf16[128,2048]{1,0:T(8,128)(2,1)S(1)} %collective-permute-done), channel_id=1, source_target_pairs={{0,4},{4,8},{8,12},{12,16},{16,20},{20,24},{24,28},{28,0},{1,5},{5... | collective-permute-start | bytes 1572872 | tf_op jit(solution)/shard_map/ppermute | solution.py:105
  75.1 13.0 %collective-permute-start.2 = (bf16[128,2048]{1,0:T(8,128)(2,1)S(1)}, bf16[128,2048]{1,0:T(8,128)(2,1)S(1)}, u32[]{:S(2)}, u32[]{:S(2)}) collective-permute-start(bf16[128,2048]{1,0:T(8,128)(2,1)S(1)} %collective-permute-done.1), channel_id=1, source_target_pairs={{0,4},{4,8},{8,12},{12,16},{16,20},{20,24},{24,28},{28,0},{1,5},{5... | collective-permute-start | bytes 1572872 | tf_op jit(solution)/shard_map/ppermute | solution.py:105
  88.1 17.8 %collective-permute-start.3 = (bf16[128,2048]{1,0:T(8,128)(2,1)S(1)}, bf16[128,2048]{1,0:T(8,128)(2,1)S(1)}, u32[]{:S(2)}, u32[]{:S(2)}) collective-permute-start(bf16[128,2048]{1,0:T(8,128)(2,1)S(1)} %collective-permute-done.2), channel_id=1, source_target_pairs={{0,4},{4,8},{8,12},{12,16},{16,20},{20,24},{24,28},{28,0},{1,5},{5... | collective-permute-start | bytes 1572872 | tf_op jit(solution)/shard_map/ppermute | solution.py:105
  105.9 22.3 %collective-permute-start.4 = (bf16[128,2048]{1,0:T(8,128)(2,1)S(1)}, bf16[128,2048]{1,0:T(8,128)(2,1)S(1)}, u32[]{:S(2)}, u32[]{:S(2)}) collective-permute-start(bf16[128,2048]{1,0:T(8,128)(2,1)S(1)} %collective-permute-done.3), channel_id=1, source_target_pairs={{0,4},{4,8},{8,12},{12,16},{16,20},{20,24},{24,28},{28,0},{1,5},{5... | collective-permute-start | bytes 1572872 | tf_op jit(solution)/shard_map/ppermute | solution.py:105
  128.2 12.1 collective-permute-start.5
  140.3 25.4 %collective-permute-start.6 = (bf16[128,2048]{1,0:T(8,128)(2,1)}, bf16[128,2048]{1,0:T(8,128)(2,1)}, u32[]{:S(2)}, u32[]{:S(2)}) collective-permute-start(bf16[128,2048]{1,0:T(8,128)(2,1)} %collective-permute-done.5), channel_id=1, source_target_pairs={{0,4},{4,8},{8,12},{12,16},{16,20},{20,24},{24,28},{28,0},{1,5},{5... | collective-permute-start | bytes 1572872 | tf_op jit(solution)/shard_map/ppermute | solution.py:105
  140.5 30.9 %copy-start.23 = (bf16[128,2048]{1,0:T(8,128)(2,1)S(1)}, bf16[128,2048]{1,0:T(8,128)(2,1)}, u32[]{:S(2)}) copy-start(bf16[128,2048]{1,0:T(8,128)(2,1)} %copy-done.22) | copy-start | bytes 1572868
  143.7 52.6 %copy-start.6 = (f32[1024,64]{1,0:T(8,128)}, f32[1024,64]{1,0:T(8,128)S(1)}, u32[]{:S(2)}) copy-start(f32[1024,64]{1,0:T(8,128)S(1)} %get-tuple-element.126) | copy-start | bytes 786436
  179.5 64.8 %copy-start.25 = (f32[2048]{0:T(1024)}, f32[2048]{0:T(1024)S(1)}, u32[]{:S(2)}) copy-start(f32[2048]{0:T(1024)S(1)} %get-tuple-element.84) | copy-start | bytes 24580
  185.8 23.2 %copy-start.10 = (bf16[1024,256]{0,1:T(8,128)(2,1)}, bf16[1024,256]{0,1:T(8,128)(2,1)S(1)}, u32[]{:S(2)}) copy-start(bf16[1024,256]{0,1:T(8,128)(2,1)S(1)} %slice.127) | copy-start | bytes 1572868
  244.3 45.5 %copy-start.35 = (f32[128]{0:T(128)}, f32[128]{0:T(128)S(1)}, u32[]{:S(2)}) copy-start(f32[128]{0:T(128)S(1)} %get-tuple-element.129) | copy-start | bytes 1540
  244.3 45.5 %copy-start.31 = (f32[128]{0:T(128)}, f32[128]{0:T(128)S(1)}, u32[]{:S(2)}) copy-start(f32[128]{0:T(128)S(1)} %fusion.88) | copy-start | bytes 1540
  246.2 516.4 %reduce-scatter.8.cloned.1.call-start = ((), (), s32[]{:S(2)}) async-start(), calls=%async_computation.12 | async-start | bytes 17301504 | tf_op jit(solution)/shard_map/reduce_scatter | solution.py:193
  580.0 182.6 %copy-start.1 = (f32[128,2048]{1,0:T(8,128)S(1)}, f32[128,2048]{1,0:T(8,128)}, u32[]{:S(2)}) copy-start(f32[128,2048]{1,0:T(8,128)} %copy-done) | copy-start | bytes 3145732
  580.0 182.6 %copy-start.26 = (f32[2048]{0:T(1024)S(1)}, f32[2048]{0:T(1024)}, u32[]{:S(2)}) copy-start(f32[2048]{0:T(1024)} %copy-done.25) | copy-start | bytes 24580
  580.1 182.6 %copy-start.32 = (f32[128]{0:T(128)S(1)}, f32[128]{0:T(128)}, u32[]{:S(2)}) copy-start(f32[128]{0:T(128)} %copy-done.31) | copy-start | bytes 1540
  580.1 184.4 %copy-start.36 = (f32[128]{0:T(128)S(1)}, f32[128]{0:T(128)}, u32[]{:S(2)}) copy-start(f32[128]{0:T(128)} %copy-done.35) | copy-start | bytes 1540
  580.1 184.4 %copy-start.9 = (bf16[1,128,2048]{2,1,0:T(8,128)(2,1)S(1)}, bf16[1,128,2048]{2,1,0:T(8,128)(2,1)}, u32[]{:S(2)}) copy-start(bf16[1,128,2048]{2,1,0:T(8,128)(2,1)} %param.14) | copy-start | bytes 1572868
  582.5 13.9 %all-to-all-start.2 = ((f32[32,2,128]{2,1,0:T(2,128)}), f32[32,2,128]{2,1,0:T(2,128)S(1)}, u32[]{:S(2)}, u32[]{:S(2)}) async-start(f32[32,2,128]{2,1,0:T(2,128)} %get-tuple-element.92), calls=%async_computation.4 | async-start | bytes 65536 | tf_op jit(solution)/shard_map/all_to_all | solution.py:198
  585.3 254.7 %all-gather.13.cloned.1.call-start = ((), (), s32[]{:S(2)}) async-start(), calls=%async_computation.13 | async-start | bytes 4718592 | tf_op jit(solution)/shard_map/all_gather | solution.py:218
  765.7 162.2 %reduce-scatter.12.cloned.1.call-start = ((), (), s32[]{:S(2)}) async-start(), calls=%async_computation.15 | async-start | bytes 7864320 | tf_op jit(solution)/shard_map/reduce_scatter | solution.py:237
  765.9 84.0 %copy-start.11 = (bf16[1024,256]{0,1:T(8,128)(2,1)S(1)}, bf16[1024,256]{0,1:T(8,128)(2,1)}, u32[]{:S(2)}) copy-start(bf16[1024,256]{0,1:T(8,128)(2,1)} %copy-done.10) | copy-start | bytes 1572868
  870.3 179.6 %reduce-scatter.10.cloned.1.call-start = ((), (), s32[]{:S(2)}) async-start(), calls=%async_computation.14 | async-start | bytes 4718592 | tf_op jit(solution)/shard_map/reduce_scatter | solution.py:232
  878.4 358.9 %reduce-scatter.6.cloned.1.call-start = ((), (), s32[]{:S(2)}) async-start(), calls=%async_computation.11 | async-start | bytes 17301504 | tf_op jit(solution)/shard_map/reduce_scatter | solution.py:202
  889.6 382.6 %reduce-scatter.14.cloned.1.call-start = ((), (), s32[]{:S(2)}) async-start(), calls=%async_computation.16 | async-start | bytes 2621440 | tf_op jit(solution)/shard_map/reduce_scatter | solution.py:220
  927.8 312.3 %all-to-all-start.3 = ((f32[8,64,768]{2,1,0:T(8,128)}), f32[8,64,768]{2,1,0:T(8,128)}, u32[]{:S(2)}, u32[]{:S(2)}) async-start(f32[8,64,768]{2,1,0:T(8,128)} %bitcast.266), calls=%async_computation.7 | async-start | bytes 3145728 | tf_op jit(solution)/shard_map/all_to_all | solution.py:238
  (29 other events, 203.4 us)
Sparse Core Ops, SparseCore 0:
  44.9 30.1 all-gather.14
  78.0 96.8 all-gather.8
  177.8 124.8 all-gather.16
  305.4 112.5 all-gather.10
  580.2 182.3 reduce-scatter.7
  765.8 74.1 all-gather.12
  870.4 57.3 reduce-scatter.11
  931.5 118.3 reduce-scatter.9
  1052.2 185.0 reduce-scatter.5
  1240.2 31.8 reduce-scatter.13
